TPU v7x, 512 devices: a whole 4x8x8 slice. The times are simulated.
512 devices in a mesh: orb: 128 (over z, y, core), pair: 4 (over x).
Axes of the slice: x: 4, y: 8, z: 8, core: 2. Of those that a mesh axis runs over, the one named last changes fastest.
Arguments:
- orbitals: float32 [256, 32, 1024], P('orb'), may hold values from -6 to 6
- send_index: int32 [128, 4, 128], P('orb', 'pair'), may hold values from -1 to 1, as said below
- pair_left: int32 [128, 4, 128], P('orb', 'pair'), may hold values from -1 to 1, as said below
- pair_offset: int32 [128, 4, 128], P('orb', 'pair'), may hold values from -8 to 8
Outputs:
- exchange_field: float32 [256, 32, 1024], P('orb', 'pair')
Inputs may be any that keep to these rules, and one draw needn't show every extreme that they name: `send_index`: -1 marks an empty route. Toward some orb index, drawn from the seed, every route from every device is live. pair_left[d, p, s + c] is -1 exactly when send_index[s, p, d + c] is -1.
All inputs are finite; a program needn't handle non-finite values.
Results may differ from a plain program's by a relative error of at most 0.0075.
Values may be sent and summed in bfloat16 or wider, within the bound.
No kernel may reach another device: no remote copies, remote signals or barrier semaphores. Data moves between devices by JAX's collectives and lax.ppermute only.
A program may use at most 128 MiB of HBM per device.

v0:
```python
import jax
import jax.numpy as jnp
from jax import lax
from jax.sharding import PartitionSpec as P

SWEEPS = 2


pair_block = 16


def in_blocks(value, dim, length):
    dims = value.shape
    pieces = value.reshape(*dims[:dim], length, dims[dim] // length, *dims[dim + 1 :])
    return jnp.moveaxis(pieces, dim, 0)


def summed_on_arrival(value, axis, dim):
    length = lax.axis_size(axis)
    pieces = lax.all_to_all(in_blocks(value, dim, length), axis, 0, 0, tiled=True)
    return jnp.sum(pieces.astype(jnp.float32), axis=0)


def neighbours(field):
    box_side = field.shape[1]
    plane = field.shape[2]
    edge_x = jnp.zeros_like(field[:, :1])
    summed = jnp.concatenate([field[:, 1:], edge_x], 1) + jnp.concatenate(
        [edge_x, field[:, :-1]], 1
    )
    edge_y = jnp.zeros_like(field[:, :, :box_side])
    summed = (
        summed
        + jnp.concatenate([field[:, :, box_side:], edge_y], 2)
        + jnp.concatenate([edge_y, field[:, :, :-box_side]], 2)
    )
    edge_z = jnp.zeros_like(field[:, :, :1])
    column = lax.broadcasted_iota(jnp.int32, (1, 1, plane), 2) % box_side
    upper = jnp.where(column < box_side - 1, jnp.concatenate([field[:, :, 1:], edge_z], 2), 0.0)
    lower = jnp.where(column > 0, jnp.concatenate([edge_z, field[:, :, :-1]], 2), 0.0)
    return summed + upper + lower


def pair_work(left, right, offsets):
    box_side = left.shape[1]
    positions = jnp.arange(box_side, dtype=jnp.int32)
    forward = (
        positions[None, None, :] == positions[None, :, None] - offsets[:, None, None]
    ).astype(jnp.bfloat16)
    shifted_right = jnp.einsum("rxw,rwc->rxc", forward, right, preferred_element_type=jnp.float32)
    left_wide = left.astype(jnp.float32)
    density = left_wide * shifted_right
    potential = jnp.zeros_like(density)
    for sweep_number in range(SWEEPS):
        potential = (neighbours(potential) + density) / 6.0
    to_left = (potential * shifted_right).astype(jnp.bfloat16)
    backward = (
        positions[None, None, :] == positions[None, :, None] + offsets[:, None, None]
    ).astype(jnp.float32)
    to_right = jnp.einsum(
        "rxw,rwc->rxc",
        backward,
        potential * left_wide,
        precision=lax.Precision.HIGHEST,
        preferred_element_type=jnp.float32,
    )
    return (to_left, to_right.astype(jnp.bfloat16))


def run_pairs(fetch, live_mask, offsets, shape):
    slot_count = live_mask.shape[0]
    keys = jnp.where(live_mask, 0, slot_count) + jnp.arange(slot_count, dtype=jnp.int32)
    arrangement = jnp.argsort(keys)
    width = min(pair_block, slot_count)
    blocks = (jnp.sum(live_mask.astype(jnp.int32)) + width - 1) // width
    empty = jnp.zeros(shape, jnp.bfloat16)

    def advance(block_number, carried):
        start = block_number * width
        chosen = lax.dynamic_slice_in_dim(arrangement, start, width, 0)
        part_left, part_right = fetch(chosen)
        out_left, out_right = pair_work(part_left, part_right, jnp.take(offsets, chosen, 0))
        return (carried[0].at[chosen].set(out_left), carried[1].at[chosen].set(out_right))

    return lax.fori_loop(0, blocks, advance, (empty, empty))


def collect(values, targets, owned):
    selector = (targets[None, :] == jnp.arange(owned, dtype=jnp.int32)[:, None]).astype(
        jnp.bfloat16
    )
    flat = values.reshape(values.shape[0], -1)
    return jnp.dot(selector, flat, preferred_element_type=jnp.float32)


def local(orbitals, send_index, pair_left, pair_offset):
    owned = orbitals.shape[0]
    box_side = orbitals.shape[1]
    plane = orbitals.shape[2]
    send_rows = send_index.reshape(-1)
    left_rows = pair_left.reshape(-1)
    offsets = pair_offset.reshape(-1)
    slot_count = send_rows.shape[0]
    n_orb = lax.axis_size("orb")
    per_peer = slot_count // n_orb
    shape = (slot_count, box_side, plane)
    rounded = orbitals.astype(jnp.bfloat16)
    padded_boxes = jnp.concatenate([rounded, jnp.zeros((1, box_side, plane), jnp.bfloat16)], 0)
    send_pick = jnp.where(send_rows >= 0, send_rows, owned)
    left_pick = jnp.where(left_rows >= 0, left_rows, owned)
    send_live = send_rows >= 0

    def local_boxes(picks, chosen):
        return jnp.take(padded_boxes, jnp.take(picks, chosen, 0), 0)

    own_left = jnp.take(padded_boxes, left_pick, 0)
    arrived, moved = (
        lax.all_to_all(
            own_left.reshape(n_orb, per_peer, box_side, plane),
            "orb",
            split_axis=0,
            concat_axis=0,
            tiled=True,
        ),
        lax.all_to_all(
            offsets.astype(jnp.bfloat16).reshape(n_orb, per_peer),
            "orb",
            split_axis=0,
            concat_axis=0,
            tiled=True,
        ),
    )
    arrived = arrived.reshape(shape)
    moved = moved.reshape(slot_count).astype(jnp.int32)

    def fetch_holder(chosen):
        return (jnp.take(arrived, chosen, 0), local_boxes(send_pick, chosen))

    to_left, to_right = run_pairs(fetch_holder, send_live, moved, shape)
    returned = lax.all_to_all(
        to_left.reshape(n_orb, per_peer, box_side, plane),
        "orb",
        split_axis=0,
        concat_axis=0,
        tiled=True,
    )
    returned = returned.reshape(shape)
    accumulated = collect(returned, left_rows, owned) + collect(to_right, send_rows, owned)
    accumulated = accumulated.reshape(owned, box_side, plane)
    field = summed_on_arrival(accumulated.astype(jnp.bfloat16), "pair", 1)
    return -0.25 * field


def solution(mesh):
    return jax.shard_map(
        local,
        mesh=mesh,
        in_specs=(
            P("orb", None, None),
            P("orb", "pair", None),
            P("orb", "pair", None),
            P("orb", "pair", None),
        ),
        out_specs=P("orb", "pair", None),
        check_vma=False,
    )
```

profile of v0, /device:TPU:152, one launch (start us, length us, event | category | flops | bytes accessed | tf_op | source)
XLA Modules:
  0.0 689.3 jit_solution(9162703989659308893)
XLA Ops:
  0.0 0.7 convert_bitcast_fusion
  0.7 0.8 copy.7
  1.4 15.5 %all-to-all-start.1 = ((bf16[128,1,1]{2,1,0:T(2,128)(2,1)}), bf16[128,1,1]{2,1,0:T(2,128)(2,1)S(1)}, u32[]{:S(2)}, u32[]{:S(2)}) async-start(bf16[128,1,1]{2,1,0:T(2,128)(2,1)} %copy.7), calls=%async_computation.1 | async-start | bytes 131072 | tf_op jit(solution)/shard_map/all_to_all | solution.py:125
  16.9 0.7 compare_and_fusion.2
  17.6 0.7 fusion.22
  18.2 1.0 convert_element_type.59
  19.2 6.4 gather_fusion.4
  25.6 7.4 %bitcast_select_fusion = bf16[128,1,32,1024]{3,2,1,0:T(8,128)(2,1)} fusion(bf16[128,32,1024]{2,1,0:T(8,128)(2,1)} %gather_fusion.4, pred[128]{0:T(512)(128)(4,1)S(1)} %compare_and_fusion.2), kind=kLoop, calls=%fused_computation.42 | loop fusion | flops 4194304 | bytes 16777344 | tf_op jit(solution)/shard_map/jit(_take)/select_n | solution.py:116
  33.0 14.3 %all-to-all-start = ((bf16[128,1,32,1024]{3,2,1,0:T(8,128)(2,1)}), bf16[128,1,32,1024]{3,2,1,0:T(8,128)(2,1)}, u32[]{:S(2)}, u32[]{:S(2)}) async-start(bf16[128,1,32,1024]{3,2,1,0:T(8,128)(2,1)} %bitcast_select_fusion), calls=%async_computation | async-start | bytes 16777216 | tf_op jit(solution)/shard_map/all_to_all | solution.py:118
  48.5 2.5 sort.17
  51.0 2.4 convert_reduce_fusion.1
  53.4 244.2 %all-to-all-done = bf16[128,1,32,1024]{3,2,1,0:T(8,128)(2,1)} async-done(((bf16[128,1,32,1024]{3,2,1,0:T(8,128)(2,1)}), bf16[128,1,32,1024]{3,2,1,0:T(8,128)(2,1)}, u32[]{:S(2)}, u32[]{:S(2)}) %all-to-all-start) | async-done | bytes 8388640 | tf_op jit(solution)/shard_map/all_to_all | solution.py:118
  297.6 4.3 broadcast_in_dim.116.clone
  301.8 4.3 broadcast_in_dim.116
  306.1 93.9 %while.14 = (s32[]{:T(128)}, bf16[128,32,1024]{2,1,0:T(8,128)(2,1)}, bf16[128,32,1024]{2,1,0:T(8,128)(2,1)}, s32[]{:T(128)}, s32[128]{0:T(128)S(1)}, /*index=5*/...) while((s32[]{:T(128)}, ...), condition=%wide.region_5.7_spmd, body=%wide.region_2.6_spmd.sunk | while | flops 249605440 | bytes 64277608 | solution.py:85
  306.3 0.7 gather_fusion.3
  306.9 0.7 gather_fusion.1
  307.7 4.0 gather_fusion
  313.5 0.8 fusion.37
  314.2 0.8 fusion.36
  315.0 2.5 multiply_convert_fusion.2
  317.5 1.4 fusion.39
  318.9 3.0 scatter_fusion
  321.9 3.0 scatter_fusion.1
  325.7 0.7 gather_fusion.1
  326.5 4.0 gather_fusion
  332.2 0.8 fusion.37
  333.0 0.8 fusion.36
  333.8 2.5 multiply_convert_fusion.2
  336.3 1.4 fusion.39
  337.7 3.0 scatter_fusion
  340.7 3.0 scatter_fusion.1
  344.4 0.7 gather_fusion.1
  345.2 4.0 gather_fusion
  351.0 0.8 fusion.37
  351.7 0.8 fusion.36
  352.5 2.5 multiply_convert_fusion.2
  355.0 1.4 fusion.39
  356.4 3.0 scatter_fusion
  359.4 3.0 scatter_fusion.1
  363.2 0.7 gather_fusion.1
  364.1 4.0 gather_fusion
  369.8 0.8 fusion.37
  370.5 0.8 fusion.36
  371.3 2.5 multiply_convert_fusion.2
  373.8 1.4 fusion.39
  375.2 3.0 scatter_fusion
  378.2 3.0 scatter_fusion.1
  382.0 0.7 gather_fusion.1
  382.8 4.0 gather_fusion
  388.5 0.8 fusion.37
  389.3 0.8 fusion.36
  390.1 2.5 multiply_convert_fusion.2
  392.6 1.4 fusion.39
  394.0 3.1 scatter_fusion
  397.0 3.0 scatter_fusion.1
  400.0 9.1 %all-to-all-start.2 = ((bf16[128,1,32,1024]{3,2,1,0:T(8,128)(2,1)}), bf16[128,1,32,1024]{3,2,1,0:T(8,128)(2,1)}, u32[]{:S(2)}, u32[]{:S(2)}) async-start(bf16[128,1,32,1024]{3,2,1,0:T(8,128)(2,1)} %bitcast.33), calls=%async_computation.2 | async-start | bytes 16777216 | tf_op jit(solution)/shard_map/all_to_all | solution.py:140
  409.1 12.6 %copy.10 = bf16[16,8,32,1024]{3,1,2,0:T(8,128)(2,1)} copy(bf16[16,8,32,1024]{3,2,1,0:T(8,128)(2,1)} %bitcast.32) | data formatting | bytes 16777216
  421.7 237.4 %all-to-all-done.2 = bf16[128,1,32,1024]{3,2,1,0:T(8,128)(2,1)} async-done(((bf16[128,1,32,1024]{3,2,1,0:T(8,128)(2,1)}), bf16[128,1,32,1024]{3,2,1,0:T(8,128)(2,1)}, u32[]{:S(2)}, u32[]{:S(2)}) %all-to-all-start.2) | async-done | bytes 8388640 | tf_op jit(solution)/shard_map/all_to_all | solution.py:140
  659.2 12.6 %copy.9 = bf16[16,8,32,1024]{3,1,2,0:T(8,128)(2,1)} copy(bf16[16,8,32,1024]{3,2,1,0:T(8,128)(2,1)} %bitcast.10) | data formatting | bytes 16777216
  671.8 4.7 fusion.16
  676.5 1.0 copy-done
  677.6 1.2 fusion.14
  678.8 9.9 %all_to_all.21 = bf16[4,2,8,1024]{3,2,1,0:T(8,128)(2,1)S(1)} all-to-all(bf16[4,2,8,1024]{3,2,1,0:T(8,128)(2,1)S(1)} %copy_bitcast_fusion.1), channel_id=1, replica_groups=mesh['orb'=128,'pair'=4] {'pair'}, dimensions={0} | all-to-all | bytes 262144 | tf_op jit(solution)/shard_map/all_to_all | solution.py:20
  (107 shorter events, 13.5 us)
Async XLA Ops:
  1.4 31.6 %all-to-all-start.1 = ((bf16[128,1,1]{2,1,0:T(2,128)(2,1)}), bf16[128,1,1]{2,1,0:T(2,128)(2,1)S(1)}, u32[]{:S(2)}, u32[]{:S(2)}) async-start(bf16[128,1,1]{2,1,0:T(2,128)(2,1)} %copy.7), calls=%async_computation.1 | async-start | bytes 131072 | tf_op jit(solution)/shard_map/all_to_all | solution.py:125
  33.0 14.3 %copy-start.1 = (s32[1,1,128]{2,1,0:T(1,128)S(1)}, s32[1,1,128]{2,1,0:T(1,128)}, u32[]{:S(2)}) copy-start(s32[1,1,128]{2,1,0:T(1,128)} %param.9) | copy-start | bytes 1540
  33.0 264.6 %all-to-all-start = ((bf16[128,1,32,1024]{3,2,1,0:T(8,128)(2,1)}), bf16[128,1,32,1024]{3,2,1,0:T(8,128)(2,1)}, u32[]{:S(2)}, u32[]{:S(2)}) async-start(bf16[128,1,32,1024]{3,2,1,0:T(8,128)(2,1)} %bitcast_select_fusion), calls=%async_computation | async-start | bytes 16777216 | tf_op jit(solution)/shard_map/all_to_all | solution.py:118
  400.0 259.1 %all-to-all-start.2 = ((bf16[128,1,32,1024]{3,2,1,0:T(8,128)(2,1)}), bf16[128,1,32,1024]{3,2,1,0:T(8,128)(2,1)}, u32[]{:S(2)}, u32[]{:S(2)}) async-start(bf16[128,1,32,1024]{3,2,1,0:T(8,128)(2,1)} %bitcast.33), calls=%async_computation.2 | async-start | bytes 16777216 | tf_op jit(solution)/shard_map/all_to_all | solution.py:140
  659.2 12.6 %copy-start.2 = (s32[1,1,128]{2,1,0:T(1,128)S(1)}, s32[1,1,128]{2,1,0:T(1,128)}, u32[]{:S(2)}) copy-start(s32[1,1,128]{2,1,0:T(1,128)} %param.10) | copy-start | bytes 1540
  671.8 5.8 copy-start
where the time goes:
time: 691 us; the launch traced here: 689 us
  waiting for transfers between devices  482 us (70%)
  local copies, waits for them, and re-layouts  112 us (16%)
  starting transfers between devices  38.8 us (6%)
  other arithmetic  29.9 us (4%)
  matrix products  16.2 us (2%)
  blocking collectives  9.86 us (1%)
    all_to_all x1, waiting for transfers between devices, local(): lax.all_to_all(own_left.reshape(n_orb, per_peer, box_side, plane), 'orb',...  244 us
    all_to_all x1, waiting for transfers between devices, local(): lax.all_to_all(to_left.reshape(n_orb, per_peer, box_side, plane), 'orb',...  237 us
    unnamed x8, local copies, waits for them, and re-layouts  26.3 us
    gather x5, local copies, waits for them, and re-layouts, fetch_holder(): return (jnp.take(arrived, chosen, 0), local_boxes(send_pick, chosen))  20 us
    all_to_all x1, starting transfers between devices, local(): lax.all_to_all(offsets.astype(jnp.bfloat16).reshape(n_orb, per_peer), 'or...  15.5 us
    scatter x5, local copies, waits for them, and re-layouts, advance(): carried[0].at[chosen].set(out_left)  15 us
    scatter x5, local copies, waits for them, and re-layouts, advance(): carried[1].at[chosen].set(out_right)  15 us
    all_to_all x1, starting transfers between devices, local(): lax.all_to_all(own_left.reshape(n_orb, per_peer, box_side, plane), 'orb',...  14.3 us
  transfers between devices with their start and end apart: 3, of which 2 were waited for; matrix products, arithmetic and copies ran while one was open for 5% of the time, Pallas kernels for 0%

commit v1 on v0

v1 whole, which is shorter than its diff:
```python
import jax
import jax.numpy as jnp
from jax import lax
from jax.experimental import pallas as pl
from jax.experimental.pallas import tpu as pltpu
from jax.sharding import PartitionSpec as P

PAD = 8
UNROLL = 4


def exchange_kernel(box, planes, unroll):
    side = box
    stride = 2 * side + 3 * PAD + 1

    def kernel(owner_ref, where_ref, own_ref, boxes_hbm, out_ref, boxes, corr, lists, sem):
        peers = boxes_hbm.shape[0]
        tasks = owner_ref.shape[0]
        copies = [
            pltpu.make_async_copy(
                boxes_hbm.at[:, pl.ds(k * side, side)],
                boxes.at[pl.ds(0, peers), pl.ds(PAD + k * (side + PAD), side)],
                sem.at[k],
            )
            for k in range(2)
        ]
        for copy in copies:
            copy.start()

        zero = jnp.zeros((PAD, 8, 128), jnp.bfloat16)

        def clear(q, _):
            boxes[q, pl.ds(0, PAD)] = zero
            boxes[q, pl.ds(PAD + side, PAD)] = zero
            boxes[q, pl.ds(2 * PAD + 2 * side, PAD)] = zero
            boxes[q, 3 * PAD + 2 * side] = zero[0]
            return 0

        lax.fori_loop(0, peers, clear, 0)
        for x in range(stride):
            boxes[peers, x] = zero[0]
        corr[...] = jnp.zeros(corr.shape, corr.dtype)

        def append(k, counts):
            owner = owner_ref[k]
            code = where_ref[k]
            lists[0, counts[0]] = code
            lists[1, counts[1]] = code
            return (
                counts[0] + (owner == 0).astype(jnp.int32),
                counts[1] + (owner == 1).astype(jnp.int32),
            )

        counts = lax.fori_loop(0, tasks, append, (jnp.int32(0), jnp.int32(0)))
        for a in range(2):
            for u in range(unroll):
                lists[a, counts[a] + u] = peers * 128
        for copy in copies:
            copy.wait()

        lane = lax.broadcasted_iota(jnp.int32, (8, 128), 1)
        row = lax.broadcasted_iota(jnp.int32, (8, 128), 0)

        def up_y(value):
            turned = pltpu.roll(value, 96, 1)
            return jnp.where(lane < 96, turned, pltpu.roll(turned, 7, 0))

        def down_y(value):
            turned = pltpu.roll(value, 32, 1)
            return jnp.where(lane >= 32, turned, pltpu.roll(turned, 1, 0))

        def owned(a, _):
            count = jnp.where(a == 0, counts[0], counts[1])

            def group(g, _):
                at = []
                for u in range(unroll):
                    code = lists[a, g * unroll + u]
                    at.append((code >> 7, code & 127))

                def plane(u, x):
                    return boxes[at[u][0], at[u][1] + x].astype(jnp.float32)

                current = [plane(u, 0) for u in range(unroll)]
                for x in range(side):
                    following = [plane(u, x + 1) for u in range(unroll)]
                    sums = [corr[a, k, x] for k in range(4)]
                    for u in range(unroll):
                        value = current[u]
                        sums[0] = sums[0] + value * value
                        sums[1] = sums[1] + value * following[u]
                        sums[2] = sums[2] + value * up_y(value)
                        sums[3] = sums[3] + value * pltpu.roll(value, 127, 1)
                    for k in range(4):
                        corr[a, k, x] = sums[k]
                    current = following
                return 0

            lax.fori_loop(0, (count + unroll - 1) // unroll, group, 0)
            return 0

        lax.fori_loop(0, 2, owned, 0)

        keep_y = jnp.logical_not(jnp.logical_and(lane >= 96, row == 7))
        keep_z = (lane % 32) < 31

        def finish(a, _):
            before = None
            for x in range(side):
                value = own_ref[a * side + x].astype(jnp.float32)
                self_part = value * corr[a, 0, x]
                along_y = jnp.where(keep_y, corr[a, 2, x], 0.0)
                along_z = jnp.where(keep_z, corr[a, 3, x], 0.0)
                total = (
                    up_y(value) * along_y
                    + down_y(value * along_y)
                    + pltpu.roll(value, 127, 1) * along_z
                    + pltpu.roll(value * along_z, 1, 1)
                )
                if x > 0:
                    total = total + before
                if x < side - 1:
                    along_x = corr[a, 1, x]
                    total = total + own_ref[a * side + x + 1].astype(jnp.float32) * along_x
                    before = value * along_x
                out_ref[a, x] = ((self_part + total / 6.0) / 6.0).astype(out_ref.dtype)
            return 0

        lax.fori_loop(0, 2, finish, 0)

    return kernel, stride


def apply_exchange(owner, where, own, boxes, interpret=False):
    peers = boxes.shape[0]
    side = own.shape[0] // 2
    kernel, stride = exchange_kernel(side, own.shape[0], UNROLL)
    tasks = owner.shape[0]
    return pl.pallas_call(
        kernel,
        out_shape=jax.ShapeDtypeStruct((2, side, 8, 128), jnp.bfloat16),
        in_specs=[
            pl.BlockSpec(memory_space=pltpu.SMEM),
            pl.BlockSpec(memory_space=pltpu.SMEM),
            pl.BlockSpec(memory_space=pltpu.VMEM),
            pl.BlockSpec(memory_space=pl.ANY),
        ],
        out_specs=pl.BlockSpec(memory_space=pltpu.VMEM),
        scratch_shapes=[
            pltpu.VMEM((peers + 1, stride, 8, 128), jnp.bfloat16),
            pltpu.VMEM((2, 4, side, 8, 128), jnp.float32),
            pltpu.SMEM((2, tasks + UNROLL), jnp.int32),
            pltpu.SemaphoreType.DMA((2,)),
        ],
        compiler_params=pltpu.CompilerParams(vmem_limit_bytes=40 * 1024 * 1024),
        interpret=interpret,
    )(owner, where, own, boxes)


def tasks_of(send_rows, left_rows, offsets, send_in, left_in, offset_in, side):
    peer = jnp.arange(send_rows.shape[0], dtype=jnp.int32) * 128 + PAD
    step = side + PAD
    as_left = peer + send_in * step - offsets
    as_right = peer + left_in * step + offset_in
    owner = jnp.concatenate([left_rows, send_rows])
    where = jnp.concatenate([as_left, as_right])
    return owner, where


def local(orbitals, send_index, pair_left, pair_offset):
    owned, side, width = orbitals.shape
    send_rows = send_index.reshape(-1)
    left_rows = pair_left.reshape(-1)
    offsets = pair_offset.reshape(-1)
    peers = send_rows.shape[0]
    own = orbitals.astype(jnp.bfloat16).reshape(owned * side, width // 128, 128)
    meta = jnp.stack([send_rows, left_rows, offsets]).astype(jnp.bfloat16)
    meta = jnp.pad(meta, ((0, 5), (0, 0)))[None]
    payload = jnp.concatenate([own, meta], 0)
    gathered = lax.all_gather(payload, "orb", axis=0, tiled=False)
    me = lax.axis_index("orb")
    column = lax.dynamic_slice(gathered, (0, owned * side, 0, me), (peers, 1, 8, 1))
    column = column.reshape(peers, 8)[:, :3].astype(jnp.int32)
    owner, where = tasks_of(
        send_rows, left_rows, offsets, column[:, 0], column[:, 1], column[:, 2], side
    )
    partial = apply_exchange(owner, where, own, gathered)
    n_pair = lax.axis_size("pair")
    pieces = partial.reshape(owned, n_pair, side // n_pair, width // 128, 128)
    pieces = lax.all_to_all(jnp.moveaxis(pieces, 1, 0), "pair", 0, 0, tiled=True)
    field = -0.25 * jnp.sum(pieces.astype(jnp.float32), axis=0)
    return field.reshape(owned, side // n_pair, width)


def solution(mesh):
    return jax.shard_map(
        local,
        mesh=mesh,
        in_specs=(
            P("orb", None, None),
            P("orb", "pair", None),
            P("orb", "pair", None),
            P("orb", "pair", None),
        ),
        out_specs=P("orb", "pair", None),
        check_vma=False,
    )
```

time: 691 us -> 155 us (0.22)
  the two profiles are of different devices: /device:TPU:152 before, /device:TPU:16 now
where the time goes in v1:
time: 155 us
  waiting for transfers between devices  106 us (68%)
  blocking collectives  18 us (12%)
  between operations  13.4 us (9%)
  Pallas kernels  11.2 us (7%)
  other arithmetic  4.38 us (3%)
  local copies, waits for them, and re-layouts  1.96 us (1%)
    all_gather x1, waiting for transfers between devices, local(): gathered = lax.all_gather(payload, 'orb', axis=0, tiled=False)  106 us
    all_to_all x1, blocking collectives, local(): lax.all_to_all(jnp.moveaxis(pieces, 1, 0), 'pair', 0, 0, tiled=True)  18 us
    pallas_call x1, Pallas kernels, apply_exchange(): pl.pallas_call(kernel, out_shape=jax.ShapeDtypeStruct((2, side, 8, 128),...  11.2 us
  transfers between devices with their start and end apart: 1, of which 1 were waited for; matrix products, arithmetic and copies ran while one was open for 0% of the time, Pallas kernels for 0%

profile of v1, /device:TPU:16, one launch (start us, length us, event | category | flops | bytes accessed | tf_op | source)
XLA Modules:
  0.0 154.5 jit_solution(9265498499207544875)
XLA Ops:
  6.5 0.0 all-gather.3.cloned.1.call-start
  6.5 0.7 convert_bitcast_fusion.2
  7.2 1.0 convert_element_type.12
  8.2 0.7 convert_bitcast_fusion
  8.9 0.7 pad_maximum_fusion
  9.6 0.0 all-gather.3.cloned.1.call-update
  9.6 0.7 pad_add_fusion.owner_ref
  10.3 105.5 %all-gather.3.cloned.1.call-done = bf16[8320,8,128]{2,1,0:T(8,128)(2,1)} async-done(((bf16[65,8,128]{2,1,0:T(8,128)(2,1)}), bf16[8320,8,128]{2,1,0:T(8,128)(2,1)}) %all-gather.3.cloned.1.call-update) | async-done | bytes 17039376 | tf_op jit(solution)/shard_map/all_gather | solution.py:180
  115.8 1.1 constant_dynamic-slice_fusion
  116.9 0.2 copy.6
  117.1 0.7 bitcast_subtract_fusion
  117.8 11.2 %shard_map.46 = bf16[2,32,8,128]{3,2,1,0:T(8,128)(2,1)S(1)} custom-call(s32[256]{0:T(256)S(1)} %pad_add_fusion.owner_ref, s32[256]{0:T(256)S(1)} %pad_add_fusion.1.where_ref, bf16[64,8,128]{2,1,0:T(8,128)(2,1)S(1)} %bitcast.34, bf16[128,65,8,128]{3,2,1,0:T(8,128)(2,1)} %bitcast.37), custom_call_target="tpu_custom_call" | custom-call | tf_op jit(solution)/shard_map/pallas_call | solution.py:139
  129.0 18.0 %all_to_all.5 = bf16[4,2,8,8,128]{4,3,2,1,0:T(8,128)(2,1)S(1)} all-to-all(bf16[4,2,8,8,128]{4,3,2,1,0:T(8,128)(2,1)S(1)} %bitcast.39), channel_id=1, replica_groups=mesh['orb'=128,'pair'=4] {'pair'}, dimensions={0} | all-to-all | bytes 262144 | tf_op jit(solution)/shard_map/all_to_all | solution.py:190
  147.0 0.6 mul.38
  (7 shorter events, 0.1 us)
Async XLA Ops:
  6.5 109.3 %all-gather.3.cloned.1.call-start = ((), (), s32[]{:S(2)}) async-start(), calls=%async_computation.1 | async-start | bytes 17172480 | tf_op jit(solution)/shard_map/all_gather | solution.py:180
Sparse Core Ops, SparseCore 0:
  10.5 105.2 all-gather.2

commit v2 on v0

v2 whole, which is shorter than its diff:
```python
import jax
import jax.numpy as jnp
import numpy as np
from jax import lax
from jax.experimental import pallas as pl
from jax.experimental.pallas import tpu as pltpu
from jax.sharding import Mesh, PartitionSpec as P

FIELDS = 4
PAD = 8
UNROLL = 4
OWNER_BIT = 20


def tile_kernel(side):
    blocks = side // 8
    pitch = side + PAD
    reach = FIELDS * pitch

    def kernel(count_ref, code_ref, own_ref, peer_ref, out_ref, pairs):
        lane = lax.broadcasted_iota(jnp.int32, (8, 128), 1)
        row = lax.broadcasted_iota(jnp.int32, (8, 128), 0)
        zero = jnp.zeros((8, 128), jnp.float32)
        keep_z = (lane % 32) < 31

        def boxes(ref, peer, a):
            here = [
                ref[peer, pl.ds(a * side + 8 * j, 8)].astype(jnp.float32) for j in range(blocks)
            ]
            edge = ref[peer, pl.ds(2 * side + 8 * a, 8)].astype(jnp.float32)
            turned = [pltpu.roll(v, 7, 0) for v in here] + [zero]
            up_x = [jnp.where(row < 7, turned[j], turned[j + 1]) for j in range(blocks)]
            up_y = []
            for j in range(blocks):
                shift = (96 - 32 * j) % 128
                beyond = pltpu.roll(edge, shift, 1) if shift else edge
                up_y.append(jnp.where(lane < 96, pltpu.roll(here[j], 96, 1), beyond))
            up_z = [pltpu.roll(v, 127, 1) for v in here]
            return here, up_x, up_y, up_z

        def build(peer, _):
            for a in range(2):
                here, up_x, up_y, up_z = boxes(peer_ref, peer, a)
                base = pl.multiple_of((peer * 2 + a) * reach, 8)
                for k, other in enumerate((here, up_x, up_y, up_z)):
                    pairs[pl.ds(base + k * pitch, 8)] = zero
                    for j in range(blocks):
                        pairs[pl.ds(base + k * pitch + PAD + 8 * j, 8)] = here[j] * other[j]
            return 0

        peers = peer_ref.shape[0]
        lax.fori_loop(0, peers, build, 0)
        pairs[pl.ds(peers * 2 * reach, PAD)] = zero

        def finish(own, _):
            edges = []
            for a in range(2):
                first = count_ref[own, 0] if a else jnp.int32(0)
                count = count_ref[own, a]

                def add(index, sums):
                    start = code_ref[own, index] & ((1 << OWNER_BIT) - 1)
                    return [
                        sums[k * blocks + j] + pairs[pl.ds(start + k * pitch + 8 * j, 8)]
                        for k in range(FIELDS)
                        for j in range(blocks)
                    ]

                def several(g, sums):
                    for u in range(UNROLL):
                        sums = add(first + g * UNROLL + u, sums)
                    return sums

                groups = count // UNROLL
                sums = [zero] * (FIELDS * blocks)
                sums = lax.fori_loop(0, groups, several, sums)
                sums = lax.fori_loop(
                    first + groups * UNROLL, first + count, lambda i, s: add(i, s), sums
                )
                here, up_x, up_y, up_z = boxes(own_ref, own, a)
                before = zero
                for j in range(blocks):
                    self_sum, along_x, along_y, along_z = [
                        sums[k * blocks + j] for k in range(FIELDS)
                    ]
                    along_z = jnp.where(keep_z, along_z, 0.0)
                    back_x = pltpu.roll(here[j] * along_x, 1, 0)
                    back_y = here[j] * along_y
                    back_z = pltpu.roll(here[j] * along_z, 1, 1)
                    total = up_x[j] * along_x + jnp.where(row > 0, back_x, before)
                    total = total + up_y[j] * along_y
                    total = total + jnp.where(lane >= 32, pltpu.roll(back_y, 32, 1), 0.0)
                    total = total + (up_z[j] * along_z + back_z)
                    before = back_x
                    total = (here[j] * self_sum + total / 6.0) / 6.0
                    chunk = own * blocks + j
                    out_ref[chunk, pl.ds(8 * a, 8)] = total.astype(out_ref.dtype)
                    past = pltpu.roll(back_y, 32 + 32 * a, 1) / 36.0
                    if a == 0:
                        edges.append(past)
                    else:
                        both = jnp.where(lane < 32, edges[j], past)
                        out_ref[chunk, pl.ds(16, 8)] = both.astype(out_ref.dtype)
            return 0

        lax.fori_loop(0, own_ref.shape[0], finish, 0)

    return kernel


def apply_tile(counts, codes, own, peer, side, interpret=False):
    blocks = side // 8
    rows = peer.shape[0] * 2 * FIELDS * (side + PAD) + PAD
    smem = pl.BlockSpec(memory_space=pltpu.SMEM)
    vmem = pl.BlockSpec(memory_space=pltpu.VMEM)
    return pl.pallas_call(
        tile_kernel(side),
        out_shape=jax.ShapeDtypeStruct((own.shape[0] * blocks, 24, 128), jnp.bfloat16),
        in_specs=[smem, smem, vmem, vmem],
        out_specs=vmem,
        scratch_shapes=[pltpu.VMEM((rows, 128), jnp.float32)],
        compiler_params=pltpu.CompilerParams(vmem_limit_bytes=16 * 1024 * 1024),
        interpret=interpret,
    )(counts, codes, own, peer)


def tasks_of(own_meta, peer_meta, side):
    reach = FIELDS * (side + PAD)
    peers = own_meta.shape[2]
    base = jnp.arange(peers, dtype=jnp.int32)[None, :, None] * 2

    def keys(owner, partner, back):
        start = (base + partner) * reach + PAD - back
        return jnp.where(owner >= 0, (owner << OWNER_BIT) + start, 4 << OWNER_BIT)

    as_left = keys(own_meta[1], peer_meta[0], own_meta[2])
    as_right = keys(own_meta[0], peer_meta[1], -peer_meta[2])
    owners = jnp.concatenate([own_meta[1], own_meta[0]], 1).reshape(own_meta.shape[1], -1)
    codes = jnp.concatenate([as_left, as_right], 1).reshape(own_meta.shape[1], -1)
    counts = jnp.stack([jnp.sum(owners == a, 1, dtype=jnp.int32) for a in range(2)], 1)
    return counts, lax.sort(codes, dimension=1, is_stable=False)


def payload_of(rounded, meta, slab):
    owned, side, width = rounded.shape
    wide = jnp.pad(rounded, ((0, 0), (0, 0), (0, 128)))
    part = lax.dynamic_slice(wide, (0, 0, slab * 128), (owned, side, 128 + side))
    edge = part[:, :, 128:].reshape(owned, side // 8, 8, side)
    edge = jnp.moveaxis(edge, 1, 2).reshape(owned * 8, 128)
    return jnp.concatenate([part[:, :, :128].reshape(owned * side, 128), edge, meta], 0)


def meta_of(received, kinds, pairs):
    meta = received[:, 80 : 80 + kinds * pairs].astype(jnp.int32)
    return meta.reshape(received.shape[0], pairs, kinds, 128)


def local(orbitals, send_index, pair_left, pair_offset):
    owned, side, width = orbitals.shape
    pairs = lax.axis_size("x")
    cores = lax.axis_size("c")
    z_size = lax.axis_size("z")
    y_size = lax.axis_size("y")
    x = lax.axis_index("x")
    y = lax.axis_index("y")
    z = lax.axis_index("z")
    rounded = orbitals.astype(jnp.bfloat16)
    meta = jnp.stack([send_index.reshape(-1), pair_left.reshape(-1), pair_offset.reshape(-1)])
    meta = jnp.broadcast_to(meta.astype(jnp.bfloat16)[None], (pairs, 3, 128))
    meta = lax.all_to_all(meta, "x", 0, 0, tiled=True).reshape(pairs * 3, 128)
    meta = jnp.pad(meta, ((0, 4), (0, 0)))
    payload = jnp.stack([payload_of(rounded, meta, c * pairs + x) for c in range(cores)])
    to_peers = jnp.broadcast_to(payload[None], (y_size,) + payload.shape)
    to_peers = to_peers.reshape((y_size * cores,) + payload.shape[1:])
    own = lax.all_to_all(to_peers, ("z", "c"), 0, 0, tiled=True)
    peer = lax.all_to_all(to_peers, ("y", "c"), 0, 0, tiled=True)

    own_meta = meta_of(own, 3, pairs)
    own_meta = lax.dynamic_slice_in_dim(own_meta, z * (y_size * cores), y_size * cores, 3)
    own_meta = jnp.transpose(own_meta, (2, 0, 3, 1))
    peer_meta = meta_of(peer, 3, pairs).reshape(-1, pairs, 3, z_size, y_size, cores)
    peer_meta = lax.dynamic_index_in_dim(peer_meta, y, 4, keepdims=False)
    peer_meta = peer_meta.reshape(-1, pairs, 3, z_size * cores)
    peer_meta = jnp.transpose(peer_meta, (2, 3, 0, 1))
    counts, codes = tasks_of(own_meta, peer_meta, side)

    partial = apply_tile(counts, codes, own, peer, side)
    landed = lax.all_to_all(partial, ("z", "c", "x"), 0, 0, tiled=True)
    landed = landed.reshape(z_size, cores * pairs, 24, 128).astype(jnp.float32)
    slabs = jnp.sum(landed, 0)
    field = slabs[:, :16].reshape(cores * pairs, owned, 8, 128)
    edge = slabs[:-1, 16:, : owned * 32].reshape(-1, 8, owned, 32)
    edge = jnp.moveaxis(edge, 2, 1)
    field = field + jnp.pad(edge, ((1, 0), (0, 0), (0, 0), (0, 96)))
    field = -0.25 * field
    return jnp.transpose(field, (1, 2, 0, 3)).reshape(owned, 8, width)


def solution(mesh):
    fine = Mesh(np.asarray(mesh.devices).reshape(8, 8, 2, 4), ("z", "y", "c", "x"))
    orb = ("z", "y", "c")
    return jax.shard_map(
        local,
        mesh=fine,
        in_specs=(
            P(orb, None, None),
            P(orb, "x", None),
            P(orb, "x", None),
            P(orb, "x", None),
        ),
        out_specs=P(orb, "x", None),
        check_vma=False,
    )
```

time: 691 us -> 109 us (0.16)
  the two profiles are of different devices: /device:TPU:152 before, /device:TPU:1 now
where the time goes in v2:
time: 109 us; the launch traced here: 108 us
  blocking collectives  42.8 us (39%)
  waiting for transfers between devices  16.9 us (16%)
  starting transfers between devices  14.8 us (14%)
  between operations  13.6 us (12%)
  Pallas kernels  10.5 us (10%)
  local copies, waits for them, and re-layouts  6.79 us (6%)
  other arithmetic  2.72 us (2%)
    all_to_all x1, blocking collectives, local(): peer = lax.all_to_all(to_peers, ('y', 'c'), 0, 0, tiled=True)  24.2 us
    all_to_all x1, blocking collectives, local(): landed = lax.all_to_all(partial, ('z', 'c', 'x'), 0, 0, tiled=True)  18.6 us
    all_to_all x1, waiting for transfers between devices, local(): own = lax.all_to_all(to_peers, ('z', 'c'), 0, 0, tiled=True)  14.1 us
    pallas_call x1, Pallas kernels, apply_tile(): pl.pallas_call(tile_kernel(side), out_shape=jax.ShapeDtypeStruct((own.sha...  10.5 us
    all_to_all x1, starting transfers between devices, local(): own = lax.all_to_all(to_peers, ('z', 'c'), 0, 0, tiled=True)  9.93 us
    all_to_all x1, starting transfers between devices, local(): meta = lax.all_to_all(meta, 'x', 0, 0, tiled=True).reshape(pairs * 3, 128)  4.83 us
    sort x2, local copies, waits for them, and re-layouts, tasks_of(): return (counts, lax.sort(codes, dimension=1, is_stable=False))  2.94 us
    all_to_all x1, waiting for transfers between devices, local(): meta = lax.all_to_all(meta, 'x', 0, 0, tiled=True).reshape(pairs * 3, 128)  2.84 us
  transfers between devices with their start and end apart: 2, of which 2 were waited for; matrix products, arithmetic and copies ran while one was open for 2% of the time, Pallas kernels for 0%

profile of v2, /device:TPU:1, one launch (start us, length us, event | category | flops | bytes accessed | tf_op | source)
XLA Modules:
  0.0 108.0 jit_solution(16243531044432450921)
XLA Ops:
  6.5 0.0 copy-start.2
  6.5 0.0 copy-start.1
  6.5 0.7 convert_bitcast_fusion.2
  7.2 0.0 copy-done.2
  7.2 0.0 copy-done.1
  7.3 0.6 broadcast_in_dim.8
  7.9 4.8 %all-to-all-start = ((bf16[4,3,128]{2,1,0:T(4,128)(2,1)}), bf16[4,3,128]{2,1,0:T(4,128)(2,1)S(1)}, u32[]{:S(2)}, u32[]{:S(2)}) async-start(bf16[4,3,128]{2,1,0:T(4,128)(2,1)} %broadcast_in_dim.8), calls=%async_computation | async-start | bytes 8192 | tf_op jit(solution)/shard_map/all_to_all | solution.py:170
  12.7 1.0 convert_element_type.31
  13.7 0.1 fusion.21
  13.8 0.1 reshape.84
  13.9 0.1 reshape.88
  14.0 2.8 %all-to-all-done = bf16[4,3,128]{2,1,0:T(4,128)(2,1)S(1)} async-done(((bf16[4,3,128]{2,1,0:T(4,128)(2,1)}), bf16[4,3,128]{2,1,0:T(4,128)(2,1)S(1)}, u32[]{:S(2)}, u32[]{:S(2)}) %all-to-all-start) | async-done | bytes 3104 | tf_op jit(solution)/shard_map/all_to_all | solution.py:170
  16.9 0.8 broadcast_in_dim.9
  17.7 24.2 %all_to_all.20.peer_ref = bf16[16,96,128]{2,1,0:T(8,128)(2,1)S(1)} all-to-all(bf16[16,96,128]{2,1,0:T(8,128)(2,1)} %bitcast.11), channel_id=1, replica_groups=mesh['z'=8,'y'=8,'c'=2,'x'=4] {'y','c'}, dimensions={0} | all-to-all | bytes 786432 | tf_op jit(solution)/shard_map/all_to_all | solution.py:176
  41.9 9.9 %all-to-all-start.1 = ((bf16[16,96,128]{2,1,0:T(8,128)(2,1)}), bf16[16,96,128]{2,1,0:T(8,128)(2,1)S(1)}, u32[]{:S(2)}, u32[]{:S(2)}) async-start(bf16[16,96,128]{2,1,0:T(8,128)(2,1)} %bitcast.11), calls=%async_computation.1 | async-start | bytes 786432 | tf_op jit(solution)/shard_map/all_to_all | solution.py:175
  51.8 0.0 sort.9.cloned.1.call-start
  51.9 0.3 copy.51
  52.2 14.1 %all-to-all-done.1.own_ref = bf16[16,96,128]{2,1,0:T(8,128)(2,1)S(1)} async-done(((bf16[16,96,128]{2,1,0:T(8,128)(2,1)}), bf16[16,96,128]{2,1,0:T(8,128)(2,1)S(1)}, u32[]{:S(2)}, u32[]{:S(2)}) %all-to-all-start.1) | async-done | bytes 393248 | tf_op jit(solution)/shard_map/all_to_all | solution.py:175
  66.4 0.1 dynamic-slice_bitcast_fusion
  66.5 0.1 pad_add_fusion.1
  66.6 0.1 copy.53
  66.7 0.7 copy.54
  67.3 0.0 sort.9.cloned.1.call-update
  67.4 0.2 convert_reduce_fusion.2
  67.6 0.1 copy.55.count_ref
  67.7 2.9 %sort.9.cloned.1.call-done.code_ref = s32[16,128]{1,0:T(8,128)} async-done(((s32[16,128]{1,0:T(8,128)}), s32[16,128]{1,0:T(8,128)}) %sort.9.cloned.1.call-update) | async-done | bytes 8208 | tf_op jit(solution)/shard_map/sort | solution.py:141
  70.6 0.0 copy-start
  70.6 0.7 copy-done
  71.3 10.5 %shard_map.46 = bf16[64,24,128]{2,1,0:T(8,128)(2,1)S(1)} custom-call(s32[16,2]{1,0:T(8,128)S(1)} %copy.55.count_ref, s32[16,128]{1,0:T(8,128)S(1)} %copy-done, bf16[16,96,128]{2,1,0:T(8,128)(2,1)S(1)} %all-to-all-done.1.own_ref, bf16[16,96,128]{2,1,0:T(8,128)(2,1)S(1)} %all_to_all.20.peer_ref), custom_call_target="tpu_custom_call" | custom-call | tf_op jit(solution)/shard_map/pallas_call | solution.py:116
  81.8 18.6 %all_to_all.21 = bf16[64,24,128]{2,1,0:T(8,128)(2,1)S(1)} all-to-all(bf16[64,24,128]{2,1,0:T(8,128)(2,1)S(1)} %shard_map.46), channel_id=1, replica_groups=mesh['z'=8,'y'=8,'c'=2,'x'=4] {'z','c','x'}, dimensions={0} | all-to-all | bytes 786432 | tf_op jit(solution)/shard_map/all_to_all | solution.py:188
  100.3 0.1 convert_reduce_fusion
  100.4 0.1 reshape.95
  100.5 0.6 copy_bitcast_fusion.1
  (19 shorter events, 0.3 us)
Async XLA Ops:
  6.5 0.7 copy-start.2
  6.5 0.7 copy-start.1
  7.9 9.0 %all-to-all-start = ((bf16[4,3,128]{2,1,0:T(4,128)(2,1)}), bf16[4,3,128]{2,1,0:T(4,128)(2,1)S(1)}, u32[]{:S(2)}, u32[]{:S(2)}) async-start(bf16[4,3,128]{2,1,0:T(4,128)(2,1)} %broadcast_in_dim.8), calls=%async_computation | async-start | bytes 8192 | tf_op jit(solution)/shard_map/all_to_all | solution.py:170
  41.9 24.4 %all-to-all-start.1 = ((bf16[16,96,128]{2,1,0:T(8,128)(2,1)}), bf16[16,96,128]{2,1,0:T(8,128)(2,1)S(1)}, u32[]{:S(2)}, u32[]{:S(2)}) async-start(bf16[16,96,128]{2,1,0:T(8,128)(2,1)} %bitcast.11), calls=%async_computation.1 | async-start | bytes 786432 | tf_op jit(solution)/shard_map/all_to_all | solution.py:175
  51.8 18.8 %sort.9.cloned.1.call-start = ((), (), s32[]{:S(2)}) async-start(), calls=%async_computation.4 | async-start | bytes 24608 | tf_op jit(solution)/shard_map/sort | solution.py:141
  70.6 0.7 copy-start
Sparse Core Ops, SparseCore 0:
  67.5 2.7 sort.11.cloned.1.call-done
  (1 shorter events, 0.0 us)

commit v3 on v2

--- a/solution.py
+++ b/solution.py
@@ -10,6 +10,7 @@
 PAD = 8
 UNROLL = 4
 OWNER_BIT = 20
+ENTRY_BITS = 7
 
 
 def tile_kernel(side):
@@ -59,7 +60,7 @@
                 count = count_ref[own, a]
 
                 def add(index, sums):
-                    start = code_ref[own, index] & ((1 << OWNER_BIT) - 1)
+                    start = (code_ref[own, index] & ((1 << OWNER_BIT) - 1)) >> ENTRY_BITS
                     return [
                         sums[k * blocks + j] + pairs[pl.ds(start + k * pitch + 8 * j, 8)]
                         for k in range(FIELDS)
@@ -131,14 +132,18 @@
 
     def keys(owner, partner, back):
         start = (base + partner) * reach + PAD - back
-        return jnp.where(owner >= 0, (owner << OWNER_BIT) + start, 4 << OWNER_BIT)
+        return jnp.where(owner >= 0, (owner << OWNER_BIT) + (start << ENTRY_BITS), 4 << OWNER_BIT)
 
     as_left = keys(own_meta[1], peer_meta[0], own_meta[2])
     as_right = keys(own_meta[0], peer_meta[1], -peer_meta[2])
     owners = jnp.concatenate([own_meta[1], own_meta[0]], 1).reshape(own_meta.shape[1], -1)
     codes = jnp.concatenate([as_left, as_right], 1).reshape(own_meta.shape[1], -1)
+    codes = codes + jnp.arange(codes.shape[1], dtype=jnp.int32)
     counts = jnp.stack([jnp.sum(owners == a, 1, dtype=jnp.int32) for a in range(2)], 1)
-    return counts, lax.sort(codes, dimension=1, is_stable=False)
+    rank = jnp.sum(codes[:, None, :] < codes[:, :, None], 2, dtype=jnp.int32)
+    slot = jnp.arange(codes.shape[1], dtype=jnp.int32)
+    placed = jnp.where(rank[:, None, :] == slot[None, :, None], codes[:, None, :], 0)
+    return counts, jnp.sum(placed, 2, dtype=jnp.int32)
 
 
 def payload_of(rounded, meta, slab):

time: 109 us -> 92.8 us (0.85)
  between operations: 13.6 us -> 0.18 us
  local copies, waits for them, and re-layouts: 6.79 us -> 2.51 us
  other arithmetic: 2.72 us -> 3.83 us
    sort x2 -> x0, local copies, waits for them, and re-layouts: 2.94 us -> none  [tasks_of(): return (counts, lax.sort(codes, dimension=1, is_stable=False))]
    reduce_sum x0 -> x2, other arithmetic: none -> 1.09 us  [the longest x1 0.65 us: tasks_of(): rank = jnp.sum(codes[:, None, :] < codes[:, :, None], 2, dtype=jnp.int32)]
where the time goes in v3:
time: 92.8 us; the launch traced here: 92.2 us
  blocking collectives  43.7 us (47%)
  waiting for transfers between devices  17 us (18%)
  starting transfers between devices  14.8 us (16%)
  Pallas kernels  10.3 us (11%)
  other arithmetic  3.83 us (4%)
  local copies, waits for them, and re-layouts  2.51 us (3%)
    all_to_all x1, blocking collectives, local(): peer = lax.all_to_all(to_peers, ('y', 'c'), 0, 0, tiled=True)  24.2 us
    all_to_all x1, blocking collectives, local(): landed = lax.all_to_all(partial, ('z', 'c', 'x'), 0, 0, tiled=True)  19.5 us
    all_to_all x1, waiting for transfers between devices, local(): own = lax.all_to_all(to_peers, ('z', 'c'), 0, 0, tiled=True)  14.1 us
    pallas_call x1, Pallas kernels, apply_tile(): pl.pallas_call(tile_kernel(side), out_shape=jax.ShapeDtypeStruct((own.sha...  10.3 us
    all_to_all x1, starting transfers between devices, local(): own = lax.all_to_all(to_peers, ('z', 'c'), 0, 0, tiled=True)  9.93 us
    all_to_all x1, starting transfers between devices, local(): meta = lax.all_to_all(meta, 'x', 0, 0, tiled=True).reshape(pairs * 3, 128)  4.83 us
    all_to_all x1, waiting for transfers between devices, local(): meta = lax.all_to_all(meta, 'x', 0, 0, tiled=True).reshape(pairs * 3, 128)  2.84 us
  transfers between devices with their start and end apart: 2, of which 2 were waited for; matrix products, arithmetic and copies ran while one was open for 2% of the time, Pallas kernels for 0%

profile of v3, /device:TPU:1, one launch (start us, length us, event | category | flops | bytes accessed | tf_op | source)
XLA Modules:
  0.0 92.2 jit_solution(5756045462645851867)
XLA Ops:
  0.0 0.0 copy-start.1
  0.0 0.0 copy-start
  0.0 0.7 convert_bitcast_fusion.2
  0.7 0.0 copy-done.1
  0.7 0.0 copy-done
  0.7 0.6 broadcast_in_dim.15
  1.3 4.8 %all-to-all-start = ((bf16[4,3,128]{2,1,0:T(4,128)(2,1)}), bf16[4,3,128]{2,1,0:T(4,128)(2,1)S(1)}, u32[]{:S(2)}, u32[]{:S(2)}) async-start(bf16[4,3,128]{2,1,0:T(4,128)(2,1)} %broadcast_in_dim.15), calls=%async_computation | async-start | bytes 8192 | tf_op jit(solution)/shard_map/all_to_all | solution.py:175
  6.1 1.0 %convert_element_type.34 = bf16[2,32,1024]{2,1,0:T(8,128)(2,1)S(1)} convert(f32[2,32,1024]{2,1,0:T(8,128)} %param.4) | non-fusion elementwise | flops 65536 | bytes 393216 | tf_op jit(solution)/shard_map/convert_element_type | solution.py:172
  7.2 0.1 fusion.23
  7.3 0.1 reshape.105
  7.4 0.1 reshape.109
  7.5 2.8 %all-to-all-done = bf16[4,3,128]{2,1,0:T(4,128)(2,1)S(1)} async-done(((bf16[4,3,128]{2,1,0:T(4,128)(2,1)}), bf16[4,3,128]{2,1,0:T(4,128)(2,1)S(1)}, u32[]{:S(2)}, u32[]{:S(2)}) %all-to-all-start) | async-done | bytes 3104 | tf_op jit(solution)/shard_map/all_to_all | solution.py:175
  10.3 0.8 broadcast_in_dim.16
  11.1 24.2 %all_to_all.20.peer_ref = bf16[16,96,128]{2,1,0:T(8,128)(2,1)S(1)} all-to-all(bf16[16,96,128]{2,1,0:T(8,128)(2,1)} %bitcast.11), channel_id=1, replica_groups=mesh['z'=8,'y'=8,'c'=2,'x'=4] {'y','c'}, dimensions={0} | all-to-all | bytes 786432 | tf_op jit(solution)/shard_map/all_to_all | solution.py:181
  35.3 9.9 %all-to-all-start.1 = ((bf16[16,96,128]{2,1,0:T(8,128)(2,1)}), bf16[16,96,128]{2,1,0:T(8,128)(2,1)S(1)}, u32[]{:S(2)}, u32[]{:S(2)}) async-start(bf16[16,96,128]{2,1,0:T(8,128)(2,1)} %bitcast.11), calls=%async_computation.1 | async-start | bytes 786432 | tf_op jit(solution)/shard_map/all_to_all | solution.py:180
  45.3 0.3 copy.68
  45.6 14.1 %all-to-all-done.1.own_ref = bf16[16,96,128]{2,1,0:T(8,128)(2,1)S(1)} async-done(((bf16[16,96,128]{2,1,0:T(8,128)(2,1)}), bf16[16,96,128]{2,1,0:T(8,128)(2,1)S(1)}, u32[]{:S(2)}, u32[]{:S(2)}) %all-to-all-start.1) | async-done | bytes 393248 | tf_op jit(solution)/shard_map/all_to_all | solution.py:180
  59.8 0.1 dynamic-slice_bitcast_fusion
  60.0 0.1 pad_add_fusion.1
  60.0 0.1 copy.70
  60.2 0.1 copy.71
  60.2 0.7 convert_reduce_fusion
  60.9 0.4 select_reduce_fusion.code_ref
  61.3 0.2 convert_reduce_fusion.3
  61.5 0.1 copy.73.count_ref
  61.6 10.3 %shard_map.46 = bf16[64,24,128]{2,1,0:T(8,128)(2,1)S(1)} custom-call(s32[16,2]{1,0:T(8,128)S(1)} %copy.73.count_ref, s32[16,128]{1,0:T(8,128)S(1)} %select_reduce_fusion.code_ref, bf16[16,96,128]{2,1,0:T(8,128)(2,1)S(1)} %all-to-all-done.1.own_ref, bf16[16,96,128]{2,1,0:T(8,128)(2,1)S(1)} %all_to_all.20.peer_ref), custom_call_target="tpu_custom_call" | custom-call | tf_op jit(solution)/shard_map/pallas_call | solution.py:117
  71.9 19.5 %all_to_all.21 = bf16[64,24,128]{2,1,0:T(8,128)(2,1)S(1)} all-to-all(bf16[64,24,128]{2,1,0:T(8,128)(2,1)S(1)} %shard_map.46), channel_id=1, replica_groups=mesh['z'=8,'y'=8,'c'=2,'x'=4] {'z','c','x'}, dimensions={0} | all-to-all | bytes 786432 | tf_op jit(solution)/shard_map/all_to_all | solution.py:193
  91.4 0.1 convert_reduce_fusion.1
  91.4 0.1 reshape.116
  91.6 0.6 copy_bitcast_fusion.1
  (20 shorter events, 0.3 us)
Async XLA Ops:
  0.0 0.7 copy-start.1
  0.0 0.7 copy-start
  1.3 9.0 %all-to-all-start = ((bf16[4,3,128]{2,1,0:T(4,128)(2,1)}), bf16[4,3,128]{2,1,0:T(4,128)(2,1)S(1)}, u32[]{:S(2)}, u32[]{:S(2)}) async-start(bf16[4,3,128]{2,1,0:T(4,128)(2,1)} %broadcast_in_dim.15), calls=%async_computation | async-start | bytes 8192 | tf_op jit(solution)/shard_map/all_to_all | solution.py:175
  35.3 24.4 %all-to-all-start.1 = ((bf16[16,96,128]{2,1,0:T(8,128)(2,1)}), bf16[16,96,128]{2,1,0:T(8,128)(2,1)S(1)}, u32[]{:S(2)}, u32[]{:S(2)}) async-start(bf16[16,96,128]{2,1,0:T(8,128)(2,1)} %bitcast.11), calls=%async_computation.1 | async-start | bytes 786432 | tf_op jit(solution)/shard_map/all_to_all | solution.py:180

commit v4 on v3

--- a/solution.py
+++ b/solution.py
@@ -18,17 +18,18 @@
     pitch = side + PAD
     reach = FIELDS * pitch
 
-    def kernel(count_ref, code_ref, own_ref, peer_ref, out_ref, pairs):
+    def kernel(core_ref, count_ref, code_ref, own_ref, peer_ref, out_ref, pairs):
         lane = lax.broadcasted_iota(jnp.int32, (8, 128), 1)
         row = lax.broadcasted_iota(jnp.int32, (8, 128), 0)
         zero = jnp.zeros((8, 128), jnp.float32)
         keep_z = (lane % 32) < 31
 
-        def boxes(ref, peer, a):
+        def boxes(ref, index, a):
             here = [
-                ref[peer, pl.ds(a * side + 8 * j, 8)].astype(jnp.float32) for j in range(blocks)
+                ref[(*index, pl.ds(a * side + 8 * j, 8))].astype(jnp.float32)
+                for j in range(blocks)
             ]
-            edge = ref[peer, pl.ds(2 * side + 8 * a, 8)].astype(jnp.float32)
+            edge = ref[(*index, pl.ds(2 * side + 8 * a, 8))].astype(jnp.float32)
             turned = [pltpu.roll(v, 7, 0) for v in here] + [zero]
             up_x = [jnp.where(row < 7, turned[j], turned[j + 1]) for j in range(blocks)]
             up_y = []
@@ -41,7 +42,7 @@
 
         def build(peer, _):
             for a in range(2):
-                here, up_x, up_y, up_z = boxes(peer_ref, peer, a)
+                here, up_x, up_y, up_z = boxes(peer_ref, (peer,), a)
                 base = pl.multiple_of((peer * 2 + a) * reach, 8)
                 for k, other in enumerate((here, up_x, up_y, up_z)):
                     pairs[pl.ds(base + k * pitch, 8)] = zero
@@ -78,7 +79,7 @@
                 sums = lax.fori_loop(
                     first + groups * UNROLL, first + count, lambda i, s: add(i, s), sums
                 )
-                here, up_x, up_y, up_z = boxes(own_ref, own, a)
+                here, up_x, up_y, up_z = boxes(own_ref, (own, core_ref[0]), a)
                 before = zero
                 for j in range(blocks):
                     self_sum, along_x, along_y, along_z = [
@@ -109,7 +110,7 @@
     return kernel
 
 
-def apply_tile(counts, codes, own, peer, side, interpret=False):
+def apply_tile(core, counts, codes, own, peer, side, interpret=False):
     blocks = side // 8
     rows = peer.shape[0] * 2 * FIELDS * (side + PAD) + PAD
     smem = pl.BlockSpec(memory_space=pltpu.SMEM)
@@ -117,12 +118,12 @@
     return pl.pallas_call(
         tile_kernel(side),
         out_shape=jax.ShapeDtypeStruct((own.shape[0] * blocks, 24, 128), jnp.bfloat16),
-        in_specs=[smem, smem, vmem, vmem],
+        in_specs=[smem, smem, smem, vmem, vmem],
         out_specs=vmem,
         scratch_shapes=[pltpu.VMEM((rows, 128), jnp.float32)],
         compiler_params=pltpu.CompilerParams(vmem_limit_bytes=16 * 1024 * 1024),
         interpret=interpret,
-    )(counts, codes, own, peer)
+    )(core, counts, codes, own, peer)
 
 
 def tasks_of(own_meta, peer_meta, side):
@@ -147,7 +148,7 @@
 
 
 def payload_of(rounded, meta, slab):
-    owned, side, width = rounded.shape
+    owned, side, _ = rounded.shape
     wide = jnp.pad(rounded, ((0, 0), (0, 0), (0, 128)))
     part = lax.dynamic_slice(wide, (0, 0, slab * 128), (owned, side, 128 + side))
     edge = part[:, :, 128:].reshape(owned, side // 8, 8, side)
@@ -177,10 +178,10 @@
     payload = jnp.stack([payload_of(rounded, meta, c * pairs + x) for c in range(cores)])
     to_peers = jnp.broadcast_to(payload[None], (y_size,) + payload.shape)
     to_peers = to_peers.reshape((y_size * cores,) + payload.shape[1:])
-    own = lax.all_to_all(to_peers, ("z", "c"), 0, 0, tiled=True)
     peer = lax.all_to_all(to_peers, ("y", "c"), 0, 0, tiled=True)
-
-    own_meta = meta_of(own, 3, pairs)
+    own = lax.all_gather(payload, ("z", "c"), axis=0, tiled=False)
+
+    own_meta = meta_of(own[:, 0], 3, pairs)
     own_meta = lax.dynamic_slice_in_dim(own_meta, z * (y_size * cores), y_size * cores, 3)
     own_meta = jnp.transpose(own_meta, (2, 0, 3, 1))
     peer_meta = meta_of(peer, 3, pairs).reshape(-1, pairs, 3, z_size, y_size, cores)
@@ -189,7 +190,8 @@
     peer_meta = jnp.transpose(peer_meta, (2, 3, 0, 1))
     counts, codes = tasks_of(own_meta, peer_meta, side)
 
-    partial = apply_tile(counts, codes, own, peer, side)
+    core = lax.axis_index("c").astype(jnp.int32).reshape(1)
+    partial = apply_tile(core, counts, codes, own, peer, side)
     landed = lax.all_to_all(partial, ("z", "c", "x"), 0, 0, tiled=True)
     landed = landed.reshape(z_size, cores * pairs, 24, 128).astype(jnp.float32)
     slabs = jnp.sum(landed, 0)

time: 92.8 us -> 92.7 us (level)
  starting transfers between devices: 14.8 us -> 12.1 us
  blocking collectives: 43.7 us -> 45.4 us
  Pallas kernels: 10.3 us -> 11.5 us
    all_gather x0 -> x1, blocking collectives: none -> 27.3 us  [local(): own = lax.all_gather(payload, ('z', 'c'), axis=0, tiled=False)]
    all_to_all x1 -> x0, blocking collectives: 24.2 us -> none  [local(): peer = lax.all_to_all(to_peers, ('y', 'c'), 0, 0, tiled=True)]
    all_to_all x1, starting transfers between devices: 9.93 us -> 7.27 us  [local(): peer = lax.all_to_all(to_peers, ('y', 'c'), 0, 0, tiled=True)]
    all_to_all x1, blocking collectives: 19.5 us -> 18.1 us  [local(): landed = lax.all_to_all(partial, ('z', 'c', 'x'), 0, 0, tiled=True)]
    pallas_call x1, Pallas kernels: 10.3 us -> 11.5 us  [apply_tile(): pl.pallas_call(tile_kernel(side), out_shape=jax.ShapeDtypeStruct((own.sha...]
where the time goes in v4:
time: 92.7 us; the launch traced here: 92.4 us
  blocking collectives  45.4 us (49%)
  waiting for transfers between devices  16.8 us (18%)
  starting transfers between devices  12.1 us (13%)
  Pallas kernels  11.5 us (12%)
  other arithmetic  3.83 us (4%)
  local copies, waits for them, and re-layouts  2.53 us (3%)
    all_gather x1, blocking collectives, local(): own = lax.all_gather(payload, ('z', 'c'), axis=0, tiled=False)  27.3 us
    all_to_all x1, blocking collectives, local(): landed = lax.all_to_all(partial, ('z', 'c', 'x'), 0, 0, tiled=True)  18.1 us
    all_to_all x1, waiting for transfers between devices, local(): peer = lax.all_to_all(to_peers, ('y', 'c'), 0, 0, tiled=True)  14 us
    pallas_call x1, Pallas kernels, apply_tile(): pl.pallas_call(tile_kernel(side), out_shape=jax.ShapeDtypeStruct((own.sha...  11.5 us
    all_to_all x1, starting transfers between devices, local(): peer = lax.all_to_all(to_peers, ('y', 'c'), 0, 0, tiled=True)  7.27 us
    all_to_all x1, starting transfers between devices, local(): meta = lax.all_to_all(meta, 'x', 0, 0, tiled=True).reshape(pairs * 3, 128)  4.83 us
    all_to_all x1, waiting for transfers between devices, local(): meta = lax.all_to_all(meta, 'x', 0, 0, tiled=True).reshape(pairs * 3, 128)  2.83 us
  transfers between devices with their start and end apart: 2, of which 2 were waited for; matrix products, arithmetic and copies ran while one was open for 2% of the time, Pallas kernels for 0%

profile of v4, /device:TPU:1, one launch (start us, length us, event | category | flops | bytes accessed | tf_op | source)
XLA Modules:
  0.0 92.4 jit_solution(13401195547245634519)
XLA Ops:
  0.0 0.0 copy-start.1
  0.0 0.0 copy-start
  0.0 0.7 convert_bitcast_fusion.2
  0.7 0.0 copy-done.1
  0.7 0.0 copy-done
  0.7 0.6 broadcast_in_dim.15
  1.3 4.8 %all-to-all-start = ((bf16[4,3,128]{2,1,0:T(4,128)(2,1)}), bf16[4,3,128]{2,1,0:T(4,128)(2,1)S(1)}, u32[]{:S(2)}, u32[]{:S(2)}) async-start(bf16[4,3,128]{2,1,0:T(4,128)(2,1)} %broadcast_in_dim.15), calls=%async_computation | async-start | bytes 8192 | tf_op jit(solution)/shard_map/all_to_all | solution.py:176
  6.1 1.0 %convert_element_type.34 = bf16[2,32,1024]{2,1,0:T(8,128)(2,1)S(1)} convert(f32[2,32,1024]{2,1,0:T(8,128)} %param.4) | non-fusion elementwise | flops 65536 | bytes 393216 | tf_op jit(solution)/shard_map/convert_element_type | solution.py:173
  7.2 0.1 fusion.23
  7.3 0.1 reshape.109
  7.4 0.1 reshape.113
  7.5 2.8 %all-to-all-done = bf16[4,3,128]{2,1,0:T(4,128)(2,1)S(1)} async-done(((bf16[4,3,128]{2,1,0:T(4,128)(2,1)}), bf16[4,3,128]{2,1,0:T(4,128)(2,1)S(1)}, u32[]{:S(2)}, u32[]{:S(2)}) %all-to-all-start) | async-done | bytes 3104 | tf_op jit(solution)/shard_map/all_to_all | solution.py:176
  10.3 27.3 %all-gather = bf16[32,96,128]{2,1,0:T(8,128)(2,1)S(1)} all-gather(bf16[2,96,128]{2,1,0:T(8,128)(2,1)S(1)} %pad_maximum_fusion), channel_id=2, replica_groups=mesh['z'=8,'y'=8,'c'=2,'x'=4] {'z','c'}, dimensions={0}, use_global_device_ids=true | all-gather | bytes 835584 | tf_op jit(solution)/shard_map/all_gather | solution.py:182
  37.6 0.8 broadcast_in_dim.16
  38.4 7.3 %all-to-all-start.1 = ((bf16[16,96,128]{2,1,0:T(8,128)(2,1)}), bf16[16,96,128]{2,1,0:T(8,128)(2,1)S(1)}, u32[]{:S(2)}, u32[]{:S(2)}) async-start(bf16[16,96,128]{2,1,0:T(8,128)(2,1)} %bitcast.20), calls=%async_computation.1 | async-start | bytes 786432 | tf_op jit(solution)/shard_map/all_to_all | solution.py:181
  45.7 0.1 dynamic-slice_bitcast_fusion
  45.9 0.2 convert_reduce_fusion.3
  46.1 0.1 copy.74.count_ref
  46.2 14.0 %all-to-all-done.1.peer_ref = bf16[16,96,128]{2,1,0:T(8,128)(2,1)S(1)} async-done(((bf16[16,96,128]{2,1,0:T(8,128)(2,1)}), bf16[16,96,128]{2,1,0:T(8,128)(2,1)S(1)}, u32[]{:S(2)}, u32[]{:S(2)}) %all-to-all-start.1) | async-done | bytes 393248 | tf_op jit(solution)/shard_map/all_to_all | solution.py:181
  60.2 0.3 copy.69
  60.5 0.1 pad_add_fusion.1
  60.6 0.1 copy.71
  60.7 0.1 copy.72
  60.8 0.7 convert_reduce_fusion
  61.4 0.4 select_reduce_fusion.code_ref
  61.9 11.5 %shard_map.46 = bf16[64,24,128]{2,1,0:T(8,128)(2,1)S(1)} custom-call(s32[1]{0:T(128)} %bitcast.core_ref, s32[16,2]{1,0:T(8,128)S(1)} %copy.74.count_ref, s32[16,128]{1,0:T(8,128)S(1)} %select_reduce_fusion.code_ref, bf16[16,2,96,128]{3,2,1,0:T(8,128)(2,1)S(1)} %bitcast.109, bf16[16,96,128]{2,1,0:T(8,128)(2,1)S(1)} %all-to-all-done.1.peer_ref), custom_call_target="tpu_custom_call" | custom-call | tf_op jit(solution)/shard_map/pallas_call | solution.py:118
  73.4 18.1 %all_to_all.15 = bf16[64,24,128]{2,1,0:T(8,128)(2,1)S(1)} all-to-all(bf16[64,24,128]{2,1,0:T(8,128)(2,1)S(1)} %shard_map.46), channel_id=1, replica_groups=mesh['z'=8,'y'=8,'c'=2,'x'=4] {'z','c','x'}, dimensions={0} | all-to-all | bytes 786432 | tf_op jit(solution)/shard_map/all_to_all | solution.py:195
  91.5 0.1 convert_reduce_fusion.1
  91.6 0.1 reshape.120
  91.7 0.6 copy_bitcast_fusion.1
  (20 shorter events, 0.3 us)
Async XLA Ops:
  0.0 0.7 copy-start.1
  0.0 0.7 copy-start
  1.3 9.0 %all-to-all-start = ((bf16[4,3,128]{2,1,0:T(4,128)(2,1)}), bf16[4,3,128]{2,1,0:T(4,128)(2,1)S(1)}, u32[]{:S(2)}, u32[]{:S(2)}) async-start(bf16[4,3,128]{2,1,0:T(4,128)(2,1)} %broadcast_in_dim.15), calls=%async_computation | async-start | bytes 8192 | tf_op jit(solution)/shard_map/all_to_all | solution.py:176
  38.4 21.8 %all-to-all-start.1 = ((bf16[16,96,128]{2,1,0:T(8,128)(2,1)}), bf16[16,96,128]{2,1,0:T(8,128)(2,1)S(1)}, u32[]{:S(2)}, u32[]{:S(2)}) async-start(bf16[16,96,128]{2,1,0:T(8,128)(2,1)} %bitcast.20), calls=%async_computation.1 | async-start | bytes 786432 | tf_op jit(solution)/shard_map/all_to_all | solution.py:181

commit v5 on v4

--- a/solution.py
+++ b/solution.py
@@ -8,7 +8,9 @@
 
 FIELDS = 4
 PAD = 8
-UNROLL = 4
+UNROLL = 8
+BUILD_STEP = 4
+FINISH_STEP = 4
 OWNER_BIT = 20
 ENTRY_BITS = 7
 
@@ -18,7 +20,7 @@
     pitch = side + PAD
     reach = FIELDS * pitch
 
-    def kernel(core_ref, count_ref, code_ref, own_ref, peer_ref, out_ref, pairs):
+    def kernel(core_ref, count_ref, code_ref, own_ref, peer_ref, out_ref, pairs, totals):
         lane = lax.broadcasted_iota(jnp.int32, (8, 128), 1)
         row = lax.broadcasted_iota(jnp.int32, (8, 128), 0)
         zero = jnp.zeros((8, 128), jnp.float32)
@@ -40,79 +42,89 @@
             up_z = [pltpu.roll(v, 127, 1) for v in here]
             return here, up_x, up_y, up_z
 
-        def build(peer, _):
-            for a in range(2):
-                here, up_x, up_y, up_z = boxes(peer_ref, (peer,), a)
-                base = pl.multiple_of((peer * 2 + a) * reach, 8)
-                for k, other in enumerate((here, up_x, up_y, up_z)):
-                    pairs[pl.ds(base + k * pitch, 8)] = zero
-                    for j in range(blocks):
-                        pairs[pl.ds(base + k * pitch + PAD + 8 * j, 8)] = here[j] * other[j]
+        def build(step, _):
+            for u in range(BUILD_STEP):
+                peer = step * BUILD_STEP + u
+                for a in range(2):
+                    here, up_x, up_y, up_z = boxes(peer_ref, (peer,), a)
+                    base = pl.multiple_of((peer * 2 + a) * reach, 8)
+                    for k, other in enumerate((here, up_x, up_y, up_z)):
+                        pairs[pl.ds(base + k * pitch, 8)] = zero
+                        for j in range(blocks):
+                            pairs[pl.ds(base + k * pitch + PAD + 8 * j, 8)] = here[j] * other[j]
             return 0
 
         peers = peer_ref.shape[0]
-        lax.fori_loop(0, peers, build, 0)
-        pairs[pl.ds(peers * 2 * reach, PAD)] = zero
-
-        def finish(own, _):
-            edges = []
+        owners = own_ref.shape[0]
+        entries = code_ref.shape[1]
+        nothing = peers * 2 * reach
+        lax.fori_loop(0, peers // BUILD_STEP, build, 0)
+        for i in range(reach // 8):
+            pairs[pl.ds(nothing + 8 * i, 8)] = zero
+
+        def gather(own, _):
             for a in range(2):
                 first = count_ref[own, 0] if a else jnp.int32(0)
-                count = count_ref[own, a]
-
-                def add(index, sums):
-                    start = (code_ref[own, index] & ((1 << OWNER_BIT) - 1)) >> ENTRY_BITS
-                    return [
-                        sums[k * blocks + j] + pairs[pl.ds(start + k * pitch + 8 * j, 8)]
-                        for k in range(FIELDS)
-                        for j in range(blocks)
-                    ]
+                last = first + count_ref[own, a]
 
                 def several(g, sums):
                     for u in range(UNROLL):
-                        sums = add(first + g * UNROLL + u, sums)
+                        index = first + g * UNROLL + u
+                        code = code_ref[own, jnp.minimum(index, entries - 1)]
+                        start = (code & ((1 << OWNER_BIT) - 1)) >> ENTRY_BITS
+                        start = jnp.where(index < last, start, nothing)
+                        sums = [
+                            sums[k * blocks + j] + pairs[pl.ds(start + k * pitch + 8 * j, 8)]
+                            for k in range(FIELDS)
+                            for j in range(blocks)
+                        ]
                     return sums
 
-                groups = count // UNROLL
-                sums = [zero] * (FIELDS * blocks)
-                sums = lax.fori_loop(0, groups, several, sums)
-                sums = lax.fori_loop(
-                    first + groups * UNROLL, first + count, lambda i, s: add(i, s), sums
-                )
-                here, up_x, up_y, up_z = boxes(own_ref, (own, core_ref[0]), a)
-                before = zero
-                for j in range(blocks):
-                    self_sum, along_x, along_y, along_z = [
-                        sums[k * blocks + j] for k in range(FIELDS)
-                    ]
-                    along_z = jnp.where(keep_z, along_z, 0.0)
-                    back_x = pltpu.roll(here[j] * along_x, 1, 0)
-                    back_y = here[j] * along_y
-                    back_z = pltpu.roll(here[j] * along_z, 1, 1)
-                    total = up_x[j] * along_x + jnp.where(row > 0, back_x, before)
-                    total = total + up_y[j] * along_y
-                    total = total + jnp.where(lane >= 32, pltpu.roll(back_y, 32, 1), 0.0)
-                    total = total + (up_z[j] * along_z + back_z)
-                    before = back_x
-                    total = (here[j] * self_sum + total / 6.0) / 6.0
-                    chunk = own * blocks + j
-                    out_ref[chunk, pl.ds(8 * a, 8)] = total.astype(out_ref.dtype)
-                    past = pltpu.roll(back_y, 32 + 32 * a, 1) / 36.0
-                    if a == 0:
-                        edges.append(past)
-                    else:
-                        both = jnp.where(lane < 32, edges[j], past)
-                        out_ref[chunk, pl.ds(16, 8)] = both.astype(out_ref.dtype)
+                groups = (last - first + UNROLL - 1) // UNROLL
+                sums = lax.fori_loop(0, groups, several, [zero] * (FIELDS * blocks))
+                for i, value in enumerate(sums):
+                    totals[own, a, i] = value
             return 0
 
-        lax.fori_loop(0, own_ref.shape[0], finish, 0)
+        lax.fori_loop(0, owners, gather, 0)
+
+        def finish(step, _):
+            for u in range(FINISH_STEP):
+                own = step * FINISH_STEP + u
+                edges = []
+                for a in range(2):
+                    here, up_x, up_y, up_z = boxes(own_ref, (own, core_ref[0]), a)
+                    before = zero
+                    for j in range(blocks):
+                        self_sum, along_x, along_y, along_z = [
+                            totals[own, a, k * blocks + j] for k in range(FIELDS)
+                        ]
+                        along_z = jnp.where(keep_z, along_z, 0.0)
+                        back_x = pltpu.roll(here[j] * along_x, 1, 0)
+                        back_y = pltpu.roll(here[j] * along_y, 32, 1)
+                        back_z = pltpu.roll(here[j] * along_z, 1, 1)
+                        total = up_x[j] * along_x + jnp.where(row > 0, back_x, before)
+                        total = total + up_y[j] * along_y + jnp.where(lane >= 32, back_y, 0.0)
+                        total = total + (up_z[j] * along_z + back_z)
+                        before = back_x
+                        total = (here[j] * self_sum + total / 6.0) / 6.0
+                        chunk = own * blocks + j
+                        out_ref[chunk, pl.ds(8 * a, 8)] = total.astype(out_ref.dtype)
+                        if a == 0:
+                            edges.append(back_y)
+                        else:
+                            both = jnp.where(lane < 32, edges[j], pltpu.roll(back_y, 32, 1))
+                            out_ref[chunk, pl.ds(16, 8)] = (both / 36.0).astype(out_ref.dtype)
+            return 0
+
+        lax.fori_loop(0, owners // FINISH_STEP, finish, 0)
 
     return kernel
 
 
 def apply_tile(core, counts, codes, own, peer, side, interpret=False):
     blocks = side // 8
-    rows = peer.shape[0] * 2 * FIELDS * (side + PAD) + PAD
+    rows = (peer.shape[0] * 2 + 1) * FIELDS * (side + PAD)
     smem = pl.BlockSpec(memory_space=pltpu.SMEM)
     vmem = pl.BlockSpec(memory_space=pltpu.VMEM)
     return pl.pallas_call(
@@ -120,7 +132,10 @@
         out_shape=jax.ShapeDtypeStruct((own.shape[0] * blocks, 24, 128), jnp.bfloat16),
         in_specs=[smem, smem, smem, vmem, vmem],
         out_specs=vmem,
-        scratch_shapes=[pltpu.VMEM((rows, 128), jnp.float32)],
+        scratch_shapes=[
+            pltpu.VMEM((rows, 128), jnp.float32),
+            pltpu.VMEM((own.shape[0], 2, FIELDS * blocks, 8, 128), jnp.float32),
+        ],
         compiler_params=pltpu.CompilerParams(vmem_limit_bytes=16 * 1024 * 1024),
         interpret=interpret,
     )(core, counts, codes, own, peer)

time: 92.7 us -> 90.8 us (0.980)
  Pallas kernels: 11.5 us -> 9.62 us
    pallas_call x1, Pallas kernels: 11.5 us -> 9.62 us  [apply_tile(): pl.pallas_call(tile_kernel(side), out_shape=jax.ShapeDtypeStruct((own.sha...]
where the time goes in v5:
time: 90.8 us; the launch traced here: 90.5 us
  blocking collectives  45.4 us (50%)
  waiting for transfers between devices  16.8 us (19%)
  starting transfers between devices  12.1 us (13%)
  Pallas kernels  9.62 us (11%)
  other arithmetic  3.83 us (4%)
  local copies, waits for them, and re-layouts  2.53 us (3%)
    all_gather x1, blocking collectives, local(): own = lax.all_gather(payload, ('z', 'c'), axis=0, tiled=False)  27.3 us
    all_to_all x1, blocking collectives, local(): landed = lax.all_to_all(partial, ('z', 'c', 'x'), 0, 0, tiled=True)  18.2 us
    all_to_all x1, waiting for transfers between devices, local(): peer = lax.all_to_all(to_peers, ('y', 'c'), 0, 0, tiled=True)  14 us
    pallas_call x1, Pallas kernels, apply_tile(): pl.pallas_call(tile_kernel(side), out_shape=jax.ShapeDtypeStruct((own.sha...  9.62 us
    all_to_all x1, starting transfers between devices, local(): peer = lax.all_to_all(to_peers, ('y', 'c'), 0, 0, tiled=True)  7.27 us
    all_to_all x1, starting transfers between devices, local(): meta = lax.all_to_all(meta, 'x', 0, 0, tiled=True).reshape(pairs * 3, 128)  4.83 us
    all_to_all x1, waiting for transfers between devices, local(): meta = lax.all_to_all(meta, 'x', 0, 0, tiled=True).reshape(pairs * 3, 128)  2.83 us
  transfers between devices with their start and end apart: 2, of which 2 were waited for; matrix products, arithmetic and copies ran while one was open for 2% of the time, Pallas kernels for 0%

profile of v5, /device:TPU:1, one launch (start us, length us, event | category | flops | bytes accessed | tf_op | source)
XLA Modules:
  0.0 90.5 jit_solution(3686360376489447635)
XLA Ops:
  0.0 0.0 copy-start.1
  0.0 0.0 copy-start
  0.0 0.7 convert_bitcast_fusion.2
  0.7 0.0 copy-done.1
  0.7 0.0 copy-done
  0.7 0.6 broadcast_in_dim.15
  1.3 4.8 %all-to-all-start = ((bf16[4,3,128]{2,1,0:T(4,128)(2,1)}), bf16[4,3,128]{2,1,0:T(4,128)(2,1)S(1)}, u32[]{:S(2)}, u32[]{:S(2)}) async-start(bf16[4,3,128]{2,1,0:T(4,128)(2,1)} %broadcast_in_dim.15), calls=%async_computation | async-start | bytes 8192 | tf_op jit(solution)/shard_map/all_to_all | solution.py:191
  6.1 1.0 %convert_element_type.34 = bf16[2,32,1024]{2,1,0:T(8,128)(2,1)S(1)} convert(f32[2,32,1024]{2,1,0:T(8,128)} %param.4) | non-fusion elementwise | flops 65536 | bytes 393216 | tf_op jit(solution)/shard_map/convert_element_type | solution.py:188
  7.2 0.1 fusion.23
  7.3 0.1 reshape.109
  7.4 0.1 reshape.113
  7.5 2.8 %all-to-all-done = bf16[4,3,128]{2,1,0:T(4,128)(2,1)S(1)} async-done(((bf16[4,3,128]{2,1,0:T(4,128)(2,1)}), bf16[4,3,128]{2,1,0:T(4,128)(2,1)S(1)}, u32[]{:S(2)}, u32[]{:S(2)}) %all-to-all-start) | async-done | bytes 3104 | tf_op jit(solution)/shard_map/all_to_all | solution.py:191
  10.3 27.3 %all-gather = bf16[32,96,128]{2,1,0:T(8,128)(2,1)S(1)} all-gather(bf16[2,96,128]{2,1,0:T(8,128)(2,1)S(1)} %pad_maximum_fusion), channel_id=2, replica_groups=mesh['z'=8,'y'=8,'c'=2,'x'=4] {'z','c'}, dimensions={0}, use_global_device_ids=true | all-gather | bytes 835584 | tf_op jit(solution)/shard_map/all_gather | solution.py:197
  37.6 0.8 broadcast_in_dim.16
  38.4 7.3 %all-to-all-start.1 = ((bf16[16,96,128]{2,1,0:T(8,128)(2,1)}), bf16[16,96,128]{2,1,0:T(8,128)(2,1)S(1)}, u32[]{:S(2)}, u32[]{:S(2)}) async-start(bf16[16,96,128]{2,1,0:T(8,128)(2,1)} %bitcast.20), calls=%async_computation.1 | async-start | bytes 786432 | tf_op jit(solution)/shard_map/all_to_all | solution.py:196
  45.7 0.1 dynamic-slice_bitcast_fusion
  45.9 0.2 convert_reduce_fusion.3
  46.1 0.1 copy.74.count_ref
  46.2 14.0 %all-to-all-done.1.peer_ref = bf16[16,96,128]{2,1,0:T(8,128)(2,1)S(1)} async-done(((bf16[16,96,128]{2,1,0:T(8,128)(2,1)}), bf16[16,96,128]{2,1,0:T(8,128)(2,1)S(1)}, u32[]{:S(2)}, u32[]{:S(2)}) %all-to-all-start.1) | async-done | bytes 393248 | tf_op jit(solution)/shard_map/all_to_all | solution.py:196
  60.2 0.3 copy.69
  60.5 0.1 pad_add_fusion.1
  60.6 0.1 copy.71
  60.7 0.1 copy.72
  60.8 0.7 convert_reduce_fusion
  61.4 0.4 select_reduce_fusion.code_ref
  61.9 9.6 %shard_map.46 = bf16[64,24,128]{2,1,0:T(8,128)(2,1)S(1)} custom-call(s32[1]{0:T(128)} %bitcast.core_ref, s32[16,2]{1,0:T(8,128)S(1)} %copy.74.count_ref, s32[16,128]{1,0:T(8,128)S(1)} %select_reduce_fusion.code_ref, bf16[16,2,96,128]{3,2,1,0:T(8,128)(2,1)S(1)} %bitcast.109, bf16[16,96,128]{2,1,0:T(8,128)(2,1)S(1)} %all-to-all-done.1.peer_ref), custom_call_target="tpu_custom_call" | custom-call | tf_op jit(solution)/shard_map/pallas_call | solution.py:130
  71.5 18.2 %all_to_all.15 = bf16[64,24,128]{2,1,0:T(8,128)(2,1)S(1)} all-to-all(bf16[64,24,128]{2,1,0:T(8,128)(2,1)S(1)} %shard_map.46), channel_id=1, replica_groups=mesh['z'=8,'y'=8,'c'=2,'x'=4] {'z','c','x'}, dimensions={0} | all-to-all | bytes 786432 | tf_op jit(solution)/shard_map/all_to_all | solution.py:210
  89.7 0.1 convert_reduce_fusion.1
  89.8 0.1 reshape.120
  89.9 0.6 copy_bitcast_fusion.1
  (20 shorter events, 0.3 us)
Async XLA Ops:
  0.0 0.7 copy-start.1
  0.0 0.7 copy-start
  1.3 9.0 %all-to-all-start = ((bf16[4,3,128]{2,1,0:T(4,128)(2,1)}), bf16[4,3,128]{2,1,0:T(4,128)(2,1)S(1)}, u32[]{:S(2)}, u32[]{:S(2)}) async-start(bf16[4,3,128]{2,1,0:T(4,128)(2,1)} %broadcast_in_dim.15), calls=%async_computation | async-start | bytes 8192 | tf_op jit(solution)/shard_map/all_to_all | solution.py:191
  38.4 21.8 %all-to-all-start.1 = ((bf16[16,96,128]{2,1,0:T(8,128)(2,1)}), bf16[16,96,128]{2,1,0:T(8,128)(2,1)S(1)}, u32[]{:S(2)}, u32[]{:S(2)}) async-start(bf16[16,96,128]{2,1,0:T(8,128)(2,1)} %bitcast.20), calls=%async_computation.1 | async-start | bytes 786432 | tf_op jit(solution)/shard_map/all_to_all | solution.py:196
